TPU v7x, 128 devices: a whole 4x4x4 slice. The times are simulated.
128 devices in a mesh: lat: 32 (over z, x, core), lev: 4 (over y).
Axes of the slice: x: 4, y: 4, z: 4, core: 2. Of those that a mesh axis runs over, the one named last changes fastest.
Arguments:
- grid: bfloat16 [640, 128, 4, 1280], P('lat', 'lev'), may hold values from -6 to 6
- legendre: bfloat16 [640, 640, 640], P('lat'), may hold values from -0.25 to 0.25
- vertical: bfloat16 [128, 128], P('lev'), may hold values from -0.5 to 0.5
- damping: bfloat16 [128], P('lev'), may hold values from 1 to 16
- lon_counts: int32 [640], replicated, may hold values from 160 to 1280
- wave_slots: int32 [640], replicated, may hold values from 0 to 639, as said below
Outputs:
- filtered_grid: bfloat16 [640, 128, 4, 1280], P('lat', 'lev')
Inputs may be any that keep to these rules, and one draw needn't show every extreme that they name: wave_slots is a permutation; slot g * 5 + r holds a wavenumber from r * 128 to (r + 1) * 128 - 1.
All inputs are finite; a program needn't handle non-finite values.
Results may differ from a plain program's by a relative error of at most 0.0074.
Values may be sent and summed in bfloat16 or wider, within the bound.
A program may use at most 128 MiB of HBM per device.

v0:
```python
import math
import jax
import jax.numpy as jnp
from jax import lax
from jax.sharding import PartitionSpec as P


def sent_together(arrays, axis, dim, along):
    widths = [math.prod(a.shape[along:]) for a in arrays]
    both = jnp.concatenate(
        [a.reshape(*a.shape[:along], w) for a, w in zip(arrays, widths)], axis=along
    )
    result = lax.all_gather(both, axis, axis=dim, tiled=True)
    pieces = jnp.split(result, [sum(widths[:k]) for k in range(1, len(widths))], axis=along)
    return tuple(
        (b.reshape(*result.shape[:along], *a.shape[along:]) for a, b in zip(arrays, pieces))
    )


def in_blocks(array, dim, peers):
    before, after = (array.shape[:dim], array.shape[dim + 1 :])
    return jnp.moveaxis(array.reshape(*before, peers, -1, *after), dim, 0)


def in_order(pieces, dim):
    lengths = list(pieces.shape[1:])
    lengths[dim] *= pieces.shape[0]
    return jnp.moveaxis(pieces, 0, dim).reshape(lengths)


def joined_exchange(array, axis, axes, splits, concats):
    sizes = [lax.axis_size(a) for a in axes]
    pieces = in_blocks(array, splits[0], sizes[0])
    pieces = jnp.moveaxis(in_blocks(pieces, splits[1] + 1, sizes[1]), 0, 1)
    inside = pieces.shape[2:]
    pieces = pieces.reshape(-1, *inside)
    pieces = lax.all_to_all(pieces, axis, split_axis=0, concat_axis=0, tiled=True)
    pieces = in_order(pieces.reshape(*sizes, *inside), concats[0] + 1)
    return in_order(pieces, concats[1])


def forward_build(wavenumbers, longitudes):
    points = jnp.arange(longitudes, dtype=jnp.int32)
    phase = (wavenumbers[:, None] * points[None, :] % longitudes).astype(jnp.float32) * (
        2.0 * math.pi / longitudes
    )
    scale = 1.0 / math.sqrt(longitudes)
    return jnp.stack([jnp.cos(phase) * scale, -jnp.sin(phase) * scale], axis=1).astype(jnp.bfloat16)


def inverse_build(wavenumbers, longitudes):
    points = jnp.arange(longitudes, dtype=jnp.int32)
    phase = (wavenumbers[:, None] * points[None, :] % longitudes).astype(jnp.float32) * (
        2.0 * math.pi / longitudes
    )
    scale = 1.0 / math.sqrt(longitudes)
    weight = jnp.where(wavenumbers == 0, 1.0, 2.0).astype(jnp.float32)[:, None]
    return jnp.stack(
        [jnp.cos(phase) * scale * weight, -jnp.sin(phase) * scale * weight], axis=1
    ).astype(jnp.bfloat16)


def damping_factor(degrees, damping):
    degree_values = jnp.arange(degrees).astype(jnp.float32)
    ratio = degree_values * (degree_values + 1.0) / float(degrees * (degrees - 1))
    return 1.0 / (1.0 + damping.astype(jnp.float32)[None, :] * (ratio * ratio)[:, None])


def legendre_forward(table, fourier, wavenumbers):
    degrees = table.shape[1]
    spectral = jnp.einsum("sna,srac->snrc", table, fourier, preferred_element_type=jnp.float32)
    live = (jnp.arange(degrees, dtype=jnp.int32)[None, :] >= wavenumbers[:, None]).astype(
        jnp.float32
    )
    return (spectral * live[:, :, None, None]).astype(jnp.bfloat16)


def legendre_inverse(table, mixed):
    banded = jnp.einsum("sna,snrc->srac", table, mixed, preferred_element_type=jnp.float32)
    return banded.astype(jnp.bfloat16)


def per_device(grid, legendre, vertical, damping, lon_counts, wave_slots):
    lat_rows, level_rows, fields, longitudes = grid.shape
    slot_count = wave_slots.shape[0]
    degrees = legendre.shape[1]
    own_slots = legendre.shape[0]
    forward_table = forward_build(wave_slots, longitudes)
    own_counts = lax.dynamic_slice_in_dim(lon_counts, lax.axis_index("lat") * lat_rows, lat_rows)
    fourier = jnp.einsum("mrx,alfx->mralf", forward_table, grid, preferred_element_type=jnp.float32)
    fourier = fourier.reshape(slot_count, 2, lat_rows, level_rows * fields)
    forward_kept = (2 * wave_slots[:, None] < own_counts[None, :]).astype(jnp.float32)
    fourier = (fourier * forward_kept[:, None, :, None]).astype(jnp.bfloat16)
    gathered = lax.all_to_all(
        lax.all_to_all(fourier, "lat", split_axis=0, concat_axis=2, tiled=True),
        "lev",
        split_axis=0,
        concat_axis=3,
        tiled=True,
    )
    count = gathered.shape[0]
    own_table = lax.dynamic_slice_in_dim(legendre, lax.axis_index("lev") * count, count, 0)
    own_waves = lax.dynamic_slice_in_dim(
        wave_slots, lax.axis_index("lat") * own_slots + lax.axis_index("lev") * count, count
    )
    spectral = legendre_forward(own_table, gathered, own_waves)
    all_rows, all_damping = sent_together((vertical, damping), "lev", 0, 1)
    levels = all_rows.shape[0]
    stacked = spectral.reshape(count, degrees, 2, levels, fields)
    mixed = stacked.astype(jnp.float32) + jnp.einsum(
        "snrkf,lk->snrlf", stacked, all_rows, preferred_element_type=jnp.float32
    )
    mixed = mixed * damping_factor(degrees, all_damping)[None, :, None, :, None]
    mixed = mixed.astype(jnp.bfloat16).reshape(count, degrees, 2, levels * fields)
    banded = legendre_inverse(own_table, mixed)
    returned = joined_exchange(banded, ("lat", "lev"), ("lat", "lev"), (2, 3), (0, 0))
    back_order = (
        wave_slots.reshape(lax.axis_size("lat"), lax.axis_size("lev"), count)
        .transpose(1, 0, 2)
        .reshape(slot_count)
    )
    inverse_table = inverse_build(back_order, longitudes)
    back_kept = (2 * back_order[:, None] < own_counts[None, :]).astype(jnp.bfloat16)
    returned = returned * back_kept[:, None, :, None]
    filtered_grid = jnp.einsum(
        "mrac,mrx->acx", returned, inverse_table, preferred_element_type=jnp.float32
    )
    return filtered_grid.reshape(lat_rows, level_rows, fields, longitudes).astype(jnp.bfloat16)


def solution(mesh):
    return jax.shard_map(
        per_device,
        mesh=mesh,
        in_specs=(
            P("lat", "lev", None, None),
            P("lat", None, None),
            P("lev", None),
            P("lev"),
            P(),
            P(),
        ),
        out_specs=P("lat", "lev", None, None),
        check_vma=False,
    )
```

profile of v0, /device:TPU:3, one launch (start us, length us, event | category | flops | bytes accessed | tf_op | source)
XLA Modules:
  0.0 534.7 jit_solution(11057568427985806592)
XLA Ops:
  0.0 15.9 %multiply_convert_fusion.5 = (bf16[640,1,1280]{2,0,1:T(8,128)(2,1)S(1)}, bf16[640,1,1280]{2,0,1:T(8,128)(2,1)S(1)}) fusion(s32[640]{0:T(1024)} %param.11), kind=kLoop, calls=%fused_computation.38 | loop fusion | flops 11468800 | bytes 3279360 | tf_op jit(solution)/shard_map/convert.3
  15.9 0.9 reshape.395
  16.9 12.1 %fusion.2 = f32[640,2,20,32,4]{0,3,4,2,1:T(8,128)S(1)} fusion(bf16[20,32,4,1280]{3,2,1,0:T(4,128)(2,1)} %param.6, bf16[640,1,1280]{2,0,1:T(8,128)(2,1)S(1)} %get-tuple-element.12, bf16[640,1,1280]{2,0,1:T(8,128)(2,1)S(1)} %get-tuple-element.11), kind=kOutput, calls=%fused_computation.8 | convolution fusion | flops 8395161600 | bytes 22937600 | tf_op jit(solution)/shard_map/mrx,alfx->mralf/dot_general | solution.py:90
  29.0 0.0 copy-start
  29.0 15.4 %copy.70 = f32[640,2,20,32,4]{0,1,4,3,2:T(2,128)} copy(f32[640,2,20,32,4]{0,3,4,2,1:T(8,128)S(1)} %fusion.2) | data formatting | bytes 26214400 | tf_op jit(solution)/shard_map/mrx,alfx->mralf/dot_general | solution.py:90
  44.4 0.2 broadcast_in_dim_reshape.4
  44.6 0.0 copy-done
  44.7 0.8 dynamic_slice.10
  45.4 0.1 compare_convert_fusion
  45.5 7.9 %multiply_convert_fusion.1 = bf16[640,2,20,128]{0,1,3,2:T(2,128)(2,1)} fusion(f32[640,2,20,128]{0,1,3,2:T(2,128)} %bitcast.64, f32[640,20]{0,1:T(8,128)S(1)} %get-tuple-element.14), kind=kLoop, calls=%fused_computation.5 | loop fusion | flops 6553600 | bytes 19712000 | tf_op jit(solution)/shard_map/convert_element_type | solution.py:93
  53.5 22.8 %copy.71 = bf16[640,2,20,128]{3,1,2,0:T(2,128)(2,1)} copy(bf16[640,2,20,128]{0,1,3,2:T(2,128)(2,1)} %multiply_convert_fusion.1) | data formatting | bytes 13107200 | tf_op jit(solution)/shard_map/convert_element_type | solution.py:93
  76.3 84.1 %all_to_all.41 = bf16[640,2,20,128]{3,1,2,0:T(2,128)(2,1)S(1)} all-to-all(bf16[640,2,20,128]{3,1,2,0:T(2,128)(2,1)} %copy.71), channel_id=1, replica_groups=mesh['lat'=32,'lev'=4] {'lat'}, dimensions={0} | all-to-all | bytes 13107200 | tf_op jit(solution)/shard_map/all_to_all | solution.py:95
  160.4 5.8 %copy.72 = bf16[20,2,32,20,128]{4,1,3,2,0:T(2,128)(2,1)} copy(bf16[20,2,32,20,128]{4,1,3,0,2:T(2,128)(2,1)S(1)} %bitcast.69) | data formatting | bytes 13107200 | tf_op jit(solution)/shard_map/all_to_all | solution.py:95
  166.3 0.0 copy-start.2
  166.3 0.0 copy-start.1
  166.3 5.4 %all-to-all-start.1 = ((bf16[20,2,640,128]{3,1,2,0:T(2,128)(2,1)}), bf16[20,2,640,128]{3,1,2,0:T(2,128)(2,1)}, u32[]{:S(2)}, u32[]{:S(2)}) async-start(bf16[20,2,640,128]{3,1,2,0:T(2,128)(2,1)} %bitcast.65), calls=%async_computation.1 | async-start | bytes 13107200 | tf_op jit(solution)/shard_map/all_to_all | solution.py:94
  171.7 0.1 dynamic_slice.11
  171.8 0.0 copy-done.2
  171.8 0.1 copy.76
  171.9 0.0 copy-done.1
  171.9 77.4 %all_gather.3 = bf16[128,129]{1,0:T(8,128)(2,1)S(1)} all-gather(bf16[32,129]{1,0:T(8,128)(2,1)S(1)} %pad_maximum_fusion.1), channel_id=1, replica_groups=mesh['lat'=32,'lev'=4] {'lev'}, dimensions={0}, use_global_device_ids=true | all-gather | bytes 41280 | tf_op jit(solution)/shard_map/all_gather | solution.py:13
  249.3 0.1 convert_reduce_fusion
  249.4 0.1 fusion.29
  249.4 0.1 add_divide_fusion
  249.6 0.0 all-to-all-done.1
  249.6 7.2 %copy.73 = bf16[20,2,640,128]{3,2,1,0:T(8,128)(2,1)} copy(bf16[20,2,640,128]{3,1,2,0:T(2,128)(2,1)} %all-to-all-done.1) | data formatting | bytes 13107200 | tf_op jit(solution)/shard_map/all_to_all | solution.py:94
  256.8 9.5 %copy.74 = bf16[5,2,640,4,128]{2,4,3,1,0:T(8,128)(2,1)} copy(bf16[5,2,640,4,128]{4,2,1,0,3:T(8,128)(2,1)} %bitcast.70) | data formatting | bytes 13107200 | tf_op jit(solution)/shard_map/all_to_all | solution.py:94
  266.3 11.1 %multiply_convert_fusion = bf16[5,640,2,512]{1,3,2,0:T(8,128)(2,1)} fusion(bf16[5,2,640,512]{2,3,1,0:T(8,128)(2,1)} %bitcast.72, f32[5,640]{1,0:T(8,128)S(1)} %fusion.29, bf16[20,640,640]{2,1,0:T(8,128)(2,1)} %param.7, s32[]{:T(128)S(6)} %select_n.50), kind=kOutput, calls=%fused_computation.4 | convolution fusion | flops 4200857600 | bytes 17216004 | tf_op jit(solution)/shard_map/sna,srac->snrc/dot_general | solution.py:71
  277.4 11.8 %reshape.389 = bf16[5,640,2,128,4]{1,4,3,2,0:T(4,128)(2,1)} reshape(bf16[5,640,2,512]{1,3,2,0:T(8,128)(2,1)} %multiply_convert_fusion) | data formatting | bytes 13107200 | tf_op jit(solution)/shard_map/reshape | solution.py:109
  289.2 7.9 %fusion.1 = bf16[5,640,2,128,4]{1,3,4,2,0:T(8,128)(2,1)S(1)} fusion(bf16[5,640,2,128,4]{1,4,3,2,0:T(4,128)(2,1)} %reshape.389, f32[640,128]{0,1:T(8,128)S(1)} %add_divide_fusion, bf16[128,129]{1,0:T(8,128)(2,1)S(1)} %all_gather.3), kind=kOutput, calls=%fused_computation.3 | convolution fusion | flops 851968000 | bytes 20021248 | tf_op jit(solution)/shard_map/snrkf,lk->snrlf/dot_general | solution.py:110
  297.1 28.2 %copy.78 = bf16[5,640,2,128,4]{1,2,4,3,0:T(2,128)(2,1)S(1)} copy(bf16[5,640,2,128,4]{1,3,4,2,0:T(8,128)(2,1)S(1)} %fusion.1) | data formatting | bytes 13107200 | tf_op jit(solution)/shard_map/convert_element_type | solution.py:114
  325.3 10.1 %convert_bitcast_fusion = bf16[5,2,640,512]{2,3,1,0:T(8,128)(2,1)} fusion(bf16[5,640,2,512]{1,2,3,0:T(2,128)(2,1)S(1)} %bitcast.73, bf16[20,640,640]{2,1,0:T(8,128)(2,1)} %param.7, s32[]{:T(128)S(6)} %select_n.50), kind=kOutput, calls=%fused_computation.15 | convolution fusion | flops 4197580800 | bytes 17203204 | tf_op jit(solution)/shard_map/sna,snrc->srac/dot_general | solution.py:79
  335.4 16.7 %copy.80 = bf16[5,2,640,512]{3,1,2,0:T(2,128)(2,1)} copy(bf16[5,2,640,512]{2,3,1,0:T(8,128)(2,1)} %convert_bitcast_fusion) | data formatting | bytes 13107200 | tf_op jit(solution)/shard_map/convert_element_type | solution.py:80
  352.1 7.1 %fusion.36 = (bf16[32,5,2,20,128]{4,2,3,0,1:T(2,128)(2,1)S(1)}, bf16[32,5,2,20,128]{4,2,3,0,1:T(2,128)(2,1)S(1)}, bf16[32,5,2,20,128]{4,2,3,0,1:T(2,128)(2,1)S(1)}, bf16[32,5,2,20,128]{4,2,3,0,1:T(2,128)(2,1)S(1)}) fusion(bf16[32,5,2,20,512]{4,2,3,0,1:T(2,128)(2,1)} %bitcast.67), kind=kLoop, calls=%fused_computation.62 | loop fusion | bytes 13107200 | tf_op jit(solution)/shard_map/slice
  359.2 11.0 %pad_maximum_fusion = bf16[32,20,2,20,128]{4,2,3,0,1:T(2,128)(2,1)S(1)} fusion(bf16[32,5,2,20,128]{4,2,3,0,1:T(2,128)(2,1)S(1)} %get-tuple-element.6, bf16[32,5,2,20,128]{4,2,3,0,1:T(2,128)(2,1)S(1)} %get-tuple-element.7, bf16[32,5,2,20,128]{4,2,3,0,1:T(2,128)(2,1)S(1)} %get-tuple-element.8, bf16[32,5,2,20,128]{4,2,3,0,1:T(2,128)(2,1)S(1)} %get-tuple-element.5), kind=kLoop, calls=%fused_computation.6 | loop fusion | flops 9830400 | bytes 13107200 | tf_op jit(solution)/shard_map/concatenate
  370.2 5.9 %copy.81 = bf16[32,20,2,20,128]{4,2,3,1,0:T(2,128)(2,1)} copy(bf16[32,20,2,20,128]{4,2,3,0,1:T(2,128)(2,1)S(1)} %pad_maximum_fusion) | data formatting | bytes 13107200 | tf_op jit(solution)/shard_map/concatenate
  376.0 8.1 %all-to-all-start.2 = ((bf16[128,5,2,20,128]{4,2,3,1,0:T(2,128)(2,1)}), bf16[128,5,2,20,128]{4,2,3,1,0:T(2,128)(2,1)}, u32[]{:S(2)}, u32[]{:S(2)}) async-start(bf16[128,5,2,20,128]{4,2,3,1,0:T(2,128)(2,1)} %bitcast.66), calls=%async_computation.2 | async-start | bytes 13107200 | tf_op jit(solution)/shard_map/all_to_all | solution.py:37
  384.2 0.2 copy.84
  384.4 15.2 %multiply_convert_fusion.3 = (bf16[640,1,1280]{2,0,1:T(8,128)(2,1)S(1)}, bf16[640,1,1280]{2,0,1:T(8,128)(2,1)S(1)}) fusion(f32[640]{0:T(1024)S(1)} %select_multiply_fusion, s32[640]{0:T(1024)S(1)} %broadcast_in_dim_reshape.4), kind=kLoop, calls=%fused_computation.33 | loop fusion | flops 11468800 | bytes 3281920 | tf_op jit(solution)/shard_map/convert.1
  399.5 63.9 %all-to-all-done.2 = bf16[128,5,2,20,128]{4,2,3,1,0:T(2,128)(2,1)} async-done(((bf16[128,5,2,20,128]{4,2,3,1,0:T(2,128)(2,1)}), bf16[128,5,2,20,128]{4,2,3,1,0:T(2,128)(2,1)}, u32[]{:S(2)}, u32[]{:S(2)}) %all-to-all-start.2) | async-done | bytes 6553632 | tf_op jit(solution)/shard_map/all_to_all | solution.py:37
  463.4 6.0 %copy.82 = bf16[32,4,5,2,20,128]{5,3,4,2,0,1:T(2,128)(2,1)S(1)} copy(bf16[32,4,5,2,20,128]{5,3,4,2,1,0:T(2,128)(2,1)} %bitcast.22) | data formatting | bytes 13107200 | tf_op jit(solution)/shard_map/reshape | solution.py:38
  469.5 17.0 %bitcast_multiply_fusion = bf16[640,2,20,128]{3,1,2,0:T(2,128)(2,1)} fusion(bf16[32,4,5,2,20,128]{5,3,4,2,0,1:T(2,128)(2,1)S(1)} %copy.82, bf16[640,20]{1,0:T(8,128)(2,1)S(1)} %copy.84), kind=kLoop, calls=%fused_computation.7 | loop fusion | flops 3276800 | bytes 13132800 | tf_op jit(solution)/shard_map/mul | solution.py:124
  486.5 23.5 %copy.85 = bf16[20,128,640,2]{2,3,1,0:T(2,128)(2,1)} copy(bf16[20,128,640,2]{1,3,0,2:T(2,128)(2,1)} %bitcast.68) | data formatting | bytes 13107200 | tf_op jit(solution)/shard_map/mrac,mrx->acx/dot_general | solution.py:125
  510.0 13.3 %bitcast_convert_fusion = bf16[20,32,4,1280]{3,1,2,0:T(8,128)(2,1)} fusion(bf16[20,32,4,640,2]{3,4,2,1,0:T(2,128)(2,1)} %bitcast.71, bf16[640,1,1280]{2,0,1:T(8,128)(2,1)S(1)} %get-tuple-element.10, bf16[640,1,1280]{2,0,1:T(8,128)(2,1)S(1)} %get-tuple-element.9), kind=kOutput, calls=%fused_computation | convolution fusion | flops 8393523200 | bytes 16384000 | tf_op jit(solution)/shard_map/mrac,mrx->acx/dot_general | solution.py:125
  523.3 11.4 %copy.87 = bf16[20,32,4,1280]{3,2,1,0:T(4,128)(2,1)} copy(bf16[20,32,4,1280]{3,1,2,0:T(8,128)(2,1)} %bitcast_convert_fusion) | data formatting | bytes 13107200 | tf_op jit(solution)/shard_map/convert_element_type | solution.py:128
  (5 shorter events, 0.0 us)
Async XLA Ops:
  29.0 15.6 %copy-start = (s32[640]{0:T(1024)S(1)}, s32[640]{0:T(1024)}, u32[]{:S(2)}) copy-start(s32[640]{0:T(1024)} %param.11) | copy-start | bytes 7684
  166.3 5.5 %copy-start.2 = (bf16[32]{0:T(256)(128)(2,1)S(1)}, bf16[32]{0:T(256)(128)(2,1)}, u32[]{:S(2)}) copy-start(bf16[32]{0:T(256)(128)(2,1)} %param.9) | copy-start | bytes 196
  166.3 5.6 %copy-start.1 = (bf16[32,128]{1,0:T(8,128)(2,1)S(1)}, bf16[32,128]{1,0:T(8,128)(2,1)}, u32[]{:S(2)}) copy-start(bf16[32,128]{1,0:T(8,128)(2,1)} %param.8) | copy-start | bytes 24580
  166.3 83.3 %all-to-all-start.1 = ((bf16[20,2,640,128]{3,1,2,0:T(2,128)(2,1)}), bf16[20,2,640,128]{3,1,2,0:T(2,128)(2,1)}, u32[]{:S(2)}, u32[]{:S(2)}) async-start(bf16[20,2,640,128]{3,1,2,0:T(2,128)(2,1)} %bitcast.65), calls=%async_computation.1 | async-start | bytes 13107200 | tf_op jit(solution)/shard_map/all_to_all | solution.py:94
  376.0 87.4 %all-to-all-start.2 = ((bf16[128,5,2,20,128]{4,2,3,1,0:T(2,128)(2,1)}), bf16[128,5,2,20,128]{4,2,3,1,0:T(2,128)(2,1)}, u32[]{:S(2)}, u32[]{:S(2)}) async-start(bf16[128,5,2,20,128]{4,2,3,1,0:T(2,128)(2,1)} %bitcast.66), calls=%async_computation.2 | async-start | bytes 13107200 | tf_op jit(solution)/shard_map/all_to_all | solution.py:37
where the time goes:
time: 537 us; the launch traced here: 535 us
  local copies, waits for them, and re-layouts  174 us (32%)
  blocking collectives  162 us (30%)
  other arithmetic  67.4 us (13%)
  waiting for transfers between devices  63.9 us (12%)
  matrix products  54.5 us (10%)
  starting transfers between devices  13.6 us (3%)
    all_to_all x1, blocking collectives, per_device(): lax.all_to_all(fourier, 'lat', split_axis=0, concat_axis=2, tiled=True)  84.1 us
    all_gather x1, blocking collectives, sent_together(): result = lax.all_gather(both, axis, axis=dim, tiled=True)  77.4 us
    all_to_all x1, waiting for transfers between devices, joined_exchange(): lax.all_to_all(pieces, axis, split_axis=0, concat_axis=0, tiled=True)  63.9 us
    another operation x2, other arithmetic  31.1 us
    convert_element_type x1, local copies, waits for them, and re-layouts, per_device(): mixed.astype(jnp.bfloat16).reshape(count, degrees, 2, levels * fields)  28.2 us
    dot_general x1, local copies, waits for them, and re-layouts, per_device(): jnp.einsum('mrac,mrx->acx', returned, inverse_table, preferred_element_ty...  23.5 us
    convert_element_type x1, local copies, waits for them, and re-layouts, per_device(): fourier = (fourier * forward_kept[:, None, :, None]).astype(jnp.bfloat16)  22.8 us
    mul x1, other arithmetic, per_device(): returned = returned * back_kept[:, None, :, None]  17 us
  transfers between devices with their start and end apart: 2, of which 1 were waited for; matrix products, arithmetic and copies ran while one was open for 3% of the time, Pallas kernels for 0%

commit v1 on v0

--- a/solution.py
+++ b/solution.py
@@ -91,12 +91,21 @@
     fourier = fourier.reshape(slot_count, 2, lat_rows, level_rows * fields)
     forward_kept = (2 * wave_slots[:, None] < own_counts[None, :]).astype(jnp.float32)
     fourier = (fourier * forward_kept[:, None, :, None]).astype(jnp.bfloat16)
-    gathered = lax.all_to_all(
-        lax.all_to_all(fourier, "lat", split_axis=0, concat_axis=2, tiled=True),
-        "lev",
-        split_axis=0,
-        concat_axis=3,
-        tiled=True,
+    gathered = jnp.concatenate(
+        lax.all_to_all(
+            jnp.stack(
+                jnp.split(
+                    lax.all_to_all(fourier, "lat", split_axis=0, concat_axis=2, tiled=True),
+                    lax.psum(1, axis_name="lev"),
+                    axis=0,
+                ),
+                0,
+            ),
+            "lev",
+            0,
+            0,
+        ),
+        3,
     )
     count = gathered.shape[0]
     own_table = lax.dynamic_slice_in_dim(legendre, lax.axis_index("lev") * count, count, 0)

time: 537 us -> 564 us (1.050); the launches traced: 535 us -> 555 us
  other arithmetic: 67.4 us -> 83.6 us
    all_to_all x3 -> x0, local copies, waits for them, and re-layouts: 22.5 us -> none  [the longest x2 16.7 us: per_device(): lax.all_to_all(lax.all_to_all(fourier, 'lat', split_axis=0, concat_axis=2...]
    reshape x0 -> x1, local copies, waits for them, and re-layouts: none -> 16.7 us  [per_device(): jnp.concatenate(lax.all_to_all(jnp.stack(jnp.split(lax.all_to_all(fourier...]
    another operation x2 -> x3, other arithmetic: 31.1 us -> 47.3 us
    split x0 -> x5, local copies, waits for them, and re-layouts: none -> 9.15 us  [per_device(): jnp.split(lax.all_to_all(fourier, 'lat', split_axis=0, concat_axis=2, til...]
    another operation x0 -> x1, local copies, waits for them, and re-layouts: none -> 7.1 us
    slice x1 -> x0, local copies, waits for them, and re-layouts: 7.1 us -> none
where the time goes in v1:
time: 564 us; the launch traced here: 555 us
  local copies, waits for them, and re-layouts  177 us (31%)
  blocking collectives  162 us (29%)
  other arithmetic  83.6 us (15%)
  waiting for transfers between devices  63.9 us (11%)
  matrix products  54.5 us (10%)
  starting transfers between devices  13.9 us (2%)
    all_to_all x1, blocking collectives, per_device(): lax.all_to_all(fourier, 'lat', split_axis=0, concat_axis=2, tiled=True)  84.4 us
    all_gather x1, blocking collectives, sent_together(): result = lax.all_gather(both, axis, axis=dim, tiled=True)  77.4 us
    all_to_all x1, waiting for transfers between devices, joined_exchange(): lax.all_to_all(pieces, axis, split_axis=0, concat_axis=0, tiled=True)  63.9 us
    another operation x2, other arithmetic  31.1 us
    convert_element_type x1, local copies, waits for them, and re-layouts, per_device(): mixed.astype(jnp.bfloat16).reshape(count, degrees, 2, levels * fields)  28.2 us
    dot_general x1, local copies, waits for them, and re-layouts, per_device(): jnp.einsum('mrac,mrx->acx', returned, inverse_table, preferred_element_ty...  23.5 us
    convert_element_type x1, local copies, waits for them, and re-layouts, per_device(): fourier = (fourier * forward_kept[:, None, :, None]).astype(jnp.bfloat16)  22.9 us
    mul x1, other arithmetic, per_device(): returned = returned * back_kept[:, None, :, None]  17 us
  transfers between devices with their start and end apart: 2, of which 1 were waited for; matrix products, arithmetic and copies ran while one was open for 3% of the time, Pallas kernels for 0%

profile of v1, /device:TPU:3, one launch (start us, length us, event | category | flops | bytes accessed | tf_op | source)
XLA Modules:
  0.0 555.2 jit_solution(17559517252346941394)
XLA Ops:
  0.0 15.9 %multiply_convert_fusion.5 = (bf16[640,1,1280]{2,0,1:T(8,128)(2,1)S(1)}, bf16[640,1,1280]{2,0,1:T(8,128)(2,1)S(1)}) fusion(s32[640]{0:T(1024)} %param.11), kind=kLoop, calls=%fused_computation.39 | loop fusion | flops 11468800 | bytes 3279360 | tf_op jit(solution)/shard_map/convert.3
  15.9 0.9 reshape.411
  16.9 12.1 %fusion.2 = f32[640,2,20,32,4]{0,3,4,2,1:T(8,128)S(1)} fusion(bf16[20,32,4,1280]{3,2,1,0:T(4,128)(2,1)} %param.6, bf16[640,1,1280]{2,0,1:T(8,128)(2,1)S(1)} %get-tuple-element.16, bf16[640,1,1280]{2,0,1:T(8,128)(2,1)S(1)} %get-tuple-element.15), kind=kOutput, calls=%fused_computation.9 | convolution fusion | flops 8395161600 | bytes 22937600 | tf_op jit(solution)/shard_map/mrx,alfx->mralf/dot_general | solution.py:90
  29.0 0.0 copy-start
  29.0 15.5 %copy.56 = f32[640,2,20,32,4]{0,1,4,3,2:T(2,128)} copy(f32[640,2,20,32,4]{0,3,4,2,1:T(8,128)S(1)} %fusion.2) | data formatting | bytes 26214400 | tf_op jit(solution)/shard_map/mrx,alfx->mralf/dot_general | solution.py:90
  44.5 0.2 broadcast_in_dim_reshape.4
  44.7 0.0 copy-done
  44.7 0.8 dynamic_slice.10
  45.5 0.1 compare_convert_fusion
  45.6 7.9 %multiply_convert_fusion.1 = bf16[640,2,20,128]{0,1,3,2:T(2,128)(2,1)} fusion(f32[640,2,20,128]{0,1,3,2:T(2,128)} %bitcast.65, f32[640,20]{0,1:T(8,128)S(1)} %get-tuple-element.18), kind=kLoop, calls=%fused_computation.5 | loop fusion | flops 6553600 | bytes 19712000 | tf_op jit(solution)/shard_map/convert_element_type | solution.py:93
  53.5 22.9 %copy.57 = bf16[640,2,20,128]{3,1,2,0:T(2,128)(2,1)} copy(bf16[640,2,20,128]{0,1,3,2:T(2,128)(2,1)} %multiply_convert_fusion.1) | data formatting | bytes 13107200 | tf_op jit(solution)/shard_map/convert_element_type | solution.py:93
  76.4 84.4 %all_to_all.25 = bf16[640,2,20,128]{3,1,2,0:T(2,128)(2,1)S(1)} all-to-all(bf16[640,2,20,128]{3,1,2,0:T(2,128)(2,1)} %copy.57), channel_id=1, replica_groups=mesh['lat'=32,'lev'=4] {'lat'}, dimensions={0} | all-to-all | bytes 13107200 | tf_op jit(solution)/shard_map/all_to_all | solution.py:98
  160.8 4.6 fusion.37
  165.5 1.1 copy.61
  166.6 1.1 copy.60
  167.7 1.1 copy.59
  168.9 1.1 copy.58
  170.0 16.2 %pad_maximum_fusion = bf16[4,5,2,640,128]{4,2,3,1,0:T(2,128)(2,1)} fusion(bf16[1,5,2,640,128]{4,2,3,1,0:T(2,128)(2,1)S(1)} %bitcast.70, bf16[1,5,2,640,128]{4,2,3,1,0:T(2,128)(2,1)S(1)} %bitcast.71, bf16[1,5,2,640,128]{4,2,3,1,0:T(2,128)(2,1)S(1)} %bitcast.72, bf16[1,5,2,640,128]{4,2,3,1,0:T(2,128)(2,1)S(1)} %bitcast.73), kind=kLoop, calls=%fused_computation.6 | loop fusion | flops 9830400 | bytes 13107200 | tf_op jit(solution)/shard_map/stack | solution.py:96
  186.2 0.0 copy-start.2
  186.2 0.0 copy-start.1
  186.2 5.4 all-to-all-start.1
  191.6 0.1 dynamic_slice.11
  191.7 0.0 copy-done.2
  191.7 0.1 copy.64
  191.8 0.0 copy-done.1
  191.8 77.4 %all_gather.3 = bf16[128,129]{1,0:T(8,128)(2,1)S(1)} all-gather(bf16[32,129]{1,0:T(8,128)(2,1)S(1)} %pad_maximum_fusion.2), channel_id=1, replica_groups=mesh['lat'=32,'lev'=4] {'lev'}, dimensions={0}, use_global_device_ids=true | all-gather | bytes 41280 | tf_op jit(solution)/shard_map/all_gather | solution.py:13
  269.2 0.1 convert_reduce_fusion
  269.3 0.1 fusion.29
  269.4 0.1 add_divide_fusion
  269.5 0.0 all-to-all-done.1
  269.5 16.7 %copy.62 = bf16[5,2,640,4,128]{2,4,3,1,0:T(8,128)(2,1)} copy(bf16[5,2,640,4,128]{4,1,2,0,3:T(2,128)(2,1)} %bitcast.13) | data formatting | bytes 13107200 | tf_op jit(solution)/shard_map/reshape | solution.py:94
  286.2 11.1 %multiply_convert_fusion = bf16[5,640,2,512]{1,3,2,0:T(8,128)(2,1)} fusion(bf16[5,2,640,512]{2,3,1,0:T(8,128)(2,1)} %bitcast.75, f32[5,640]{1,0:T(8,128)S(1)} %fusion.29, bf16[20,640,640]{2,1,0:T(8,128)(2,1)} %param.7, s32[]{:T(128)S(6)} %select_n.50), kind=kOutput, calls=%fused_computation.4 | convolution fusion | flops 4200857600 | bytes 17216004 | tf_op jit(solution)/shard_map/sna,srac->snrc/dot_general | solution.py:71
  297.3 11.8 %reshape.405 = bf16[5,640,2,128,4]{1,4,3,2,0:T(4,128)(2,1)} reshape(bf16[5,640,2,512]{1,3,2,0:T(8,128)(2,1)} %multiply_convert_fusion) | data formatting | bytes 13107200 | tf_op jit(solution)/shard_map/reshape | solution.py:118
  309.1 7.9 %fusion.1 = bf16[5,640,2,128,4]{1,3,4,2,0:T(8,128)(2,1)S(1)} fusion(bf16[5,640,2,128,4]{1,4,3,2,0:T(4,128)(2,1)} %reshape.405, f32[640,128]{0,1:T(8,128)S(1)} %add_divide_fusion, bf16[128,129]{1,0:T(8,128)(2,1)S(1)} %all_gather.3), kind=kOutput, calls=%fused_computation.3 | convolution fusion | flops 851968000 | bytes 20021248 | tf_op jit(solution)/shard_map/snrkf,lk->snrlf/dot_general | solution.py:119
  316.9 28.2 %copy.66 = bf16[5,640,2,128,4]{1,2,4,3,0:T(2,128)(2,1)S(1)} copy(bf16[5,640,2,128,4]{1,3,4,2,0:T(8,128)(2,1)S(1)} %fusion.1) | data formatting | bytes 13107200 | tf_op jit(solution)/shard_map/convert_element_type | solution.py:123
  345.2 10.1 %convert_bitcast_fusion = bf16[5,2,640,512]{2,3,1,0:T(8,128)(2,1)} fusion(bf16[5,640,2,512]{1,2,3,0:T(2,128)(2,1)S(1)} %bitcast.76, bf16[20,640,640]{2,1,0:T(8,128)(2,1)} %param.7, s32[]{:T(128)S(6)} %select_n.50), kind=kOutput, calls=%fused_computation.16 | convolution fusion | flops 4197580800 | bytes 17203204 | tf_op jit(solution)/shard_map/sna,snrc->srac/dot_general | solution.py:79
  355.3 16.7 %copy.68 = bf16[5,2,640,512]{3,1,2,0:T(2,128)(2,1)} copy(bf16[5,2,640,512]{2,3,1,0:T(8,128)(2,1)} %convert_bitcast_fusion) | data formatting | bytes 13107200 | tf_op jit(solution)/shard_map/convert_element_type | solution.py:80
  372.0 7.1 %fusion.36 = (bf16[32,5,2,20,128]{4,2,3,0,1:T(2,128)(2,1)S(1)}, bf16[32,5,2,20,128]{4,2,3,0,1:T(2,128)(2,1)S(1)}, bf16[32,5,2,20,128]{4,2,3,0,1:T(2,128)(2,1)S(1)}, bf16[32,5,2,20,128]{4,2,3,0,1:T(2,128)(2,1)S(1)}) fusion(bf16[32,5,2,20,512]{4,2,3,0,1:T(2,128)(2,1)} %bitcast.68), kind=kLoop, calls=%fused_computation.63 | loop fusion | bytes 13107200 | tf_op jit(solution)/shard_map/slice.4
  379.1 11.0 %pad_maximum_fusion.1 = bf16[32,20,2,20,128]{4,2,3,0,1:T(2,128)(2,1)S(1)} fusion(bf16[32,5,2,20,128]{4,2,3,0,1:T(2,128)(2,1)S(1)} %get-tuple-element.6, bf16[32,5,2,20,128]{4,2,3,0,1:T(2,128)(2,1)S(1)} %get-tuple-element.7, bf16[32,5,2,20,128]{4,2,3,0,1:T(2,128)(2,1)S(1)} %get-tuple-element.8, bf16[32,5,2,20,128]{4,2,3,0,1:T(2,128)(2,1)S(1)} %get-tuple-element.5), kind=kLoop, calls=%fused_computation.7 | loop fusion | flops 9830400 | bytes 13107200 | tf_op jit(solution)/shard_map/concatenate
  390.1 5.9 %copy.69 = bf16[32,20,2,20,128]{4,2,3,1,0:T(2,128)(2,1)} copy(bf16[32,20,2,20,128]{4,2,3,0,1:T(2,128)(2,1)S(1)} %pad_maximum_fusion.1) | data formatting | bytes 13107200 | tf_op jit(solution)/shard_map/concatenate
  396.0 8.5 %all-to-all-start.2 = ((bf16[128,5,2,20,128]{4,2,3,1,0:T(2,128)(2,1)}), bf16[128,5,2,20,128]{4,2,3,1,0:T(2,128)(2,1)}, u32[]{:S(2)}, u32[]{:S(2)}) async-start(bf16[128,5,2,20,128]{4,2,3,1,0:T(2,128)(2,1)} %bitcast.66), calls=%async_computation.2 | async-start | bytes 13107200 | tf_op jit(solution)/shard_map/all_to_all | solution.py:37
  404.5 0.2 copy.72
  404.7 15.2 %multiply_convert_fusion.3 = (bf16[640,1,1280]{2,0,1:T(8,128)(2,1)S(1)}, bf16[640,1,1280]{2,0,1:T(8,128)(2,1)S(1)}) fusion(f32[640]{0:T(1024)S(1)} %select_multiply_fusion, s32[640]{0:T(1024)S(1)} %broadcast_in_dim_reshape.4), kind=kLoop, calls=%fused_computation.34 | loop fusion | flops 11468800 | bytes 3281920 | tf_op jit(solution)/shard_map/convert.1
  419.8 63.9 %all-to-all-done.2 = bf16[128,5,2,20,128]{4,2,3,1,0:T(2,128)(2,1)} async-done(((bf16[128,5,2,20,128]{4,2,3,1,0:T(2,128)(2,1)}), bf16[128,5,2,20,128]{4,2,3,1,0:T(2,128)(2,1)}, u32[]{:S(2)}, u32[]{:S(2)}) %all-to-all-start.2) | async-done | bytes 6553632 | tf_op jit(solution)/shard_map/all_to_all | solution.py:37
  483.7 6.0 %copy.70 = bf16[32,4,5,2,20,128]{5,3,4,2,0,1:T(2,128)(2,1)S(1)} copy(bf16[32,4,5,2,20,128]{5,3,4,2,1,0:T(2,128)(2,1)} %bitcast.25) | data formatting | bytes 13107200 | tf_op jit(solution)/shard_map/reshape | solution.py:38
  489.7 17.0 %bitcast_multiply_fusion = bf16[640,2,20,128]{3,1,2,0:T(2,128)(2,1)} fusion(bf16[32,4,5,2,20,128]{5,3,4,2,0,1:T(2,128)(2,1)S(1)} %copy.70, bf16[640,20]{1,0:T(8,128)(2,1)S(1)} %copy.72), kind=kLoop, calls=%fused_computation.8 | loop fusion | flops 3276800 | bytes 13132800 | tf_op jit(solution)/shard_map/mul | solution.py:133
  506.7 23.5 %copy.73 = bf16[20,128,640,2]{2,3,1,0:T(2,128)(2,1)} copy(bf16[20,128,640,2]{1,3,0,2:T(2,128)(2,1)} %bitcast.69) | data formatting | bytes 13107200 | tf_op jit(solution)/shard_map/mrac,mrx->acx/dot_general | solution.py:134
  530.2 13.4 %bitcast_convert_fusion = bf16[20,32,4,1280]{3,1,2,0:T(8,128)(2,1)} fusion(bf16[20,32,4,640,2]{3,4,2,1,0:T(2,128)(2,1)} %bitcast.74, bf16[640,1,1280]{2,0,1:T(8,128)(2,1)S(1)} %get-tuple-element.14, bf16[640,1,1280]{2,0,1:T(8,128)(2,1)S(1)} %get-tuple-element.13), kind=kOutput, calls=%fused_computation | convolution fusion | flops 8393523200 | bytes 16384000 | tf_op jit(solution)/shard_map/mrac,mrx->acx/dot_general | solution.py:134
  543.6 11.4 %copy.75 = bf16[20,32,4,1280]{3,2,1,0:T(4,128)(2,1)} copy(bf16[20,32,4,1280]{3,1,2,0:T(8,128)(2,1)} %bitcast_convert_fusion) | data formatting | bytes 13107200 | tf_op jit(solution)/shard_map/convert_element_type | solution.py:137
  (5 shorter events, 0.0 us)
Async XLA Ops:
  29.0 15.7 %copy-start = (s32[640]{0:T(1024)S(1)}, s32[640]{0:T(1024)}, u32[]{:S(2)}) copy-start(s32[640]{0:T(1024)} %param.11) | copy-start | bytes 7684
  186.2 5.5 copy-start.2
  186.2 5.6 %copy-start.1 = (bf16[32,128]{1,0:T(8,128)(2,1)S(1)}, bf16[32,128]{1,0:T(8,128)(2,1)}, u32[]{:S(2)}) copy-start(bf16[32,128]{1,0:T(8,128)(2,1)} %param.8) | copy-start | bytes 24580
  186.2 83.3 %all-to-all-start.1 = ((bf16[4,5,2,640,128]{4,2,3,1,0:T(2,128)(2,1)}), bf16[4,5,2,640,128]{4,2,3,1,0:T(2,128)(2,1)}, u32[]{:S(2)}, u32[]{:S(2)}) async-start(bf16[4,5,2,640,128]{4,2,3,1,0:T(2,128)(2,1)} %pad_maximum_fusion), calls=%async_computation.1 | async-start | bytes 13107200 | tf_op jit(solution)/shard_map/all_to_all | solution.py:95
  396.0 87.7 %all-to-all-start.2 = ((bf16[128,5,2,20,128]{4,2,3,1,0:T(2,128)(2,1)}), bf16[128,5,2,20,128]{4,2,3,1,0:T(2,128)(2,1)}, u32[]{:S(2)}, u32[]{:S(2)}) async-start(bf16[128,5,2,20,128]{4,2,3,1,0:T(2,128)(2,1)} %bitcast.66), calls=%async_computation.2 | async-start | bytes 13107200 | tf_op jit(solution)/shard_map/all_to_all | solution.py:37
